TPU v7x, 32 devices: a whole 2x2x4 slice. The times are simulated.
32 devices in a mesh: lat: 8 (over z, y), lon: 4 (over x, core).
Axes of the slice: x: 2, y: 2, z: 4, core: 2. Of those that a mesh axis runs over, the one named last changes fastest.
Arguments:
- predicted_state: bfloat16 [222, 320, 512], P(None, 'lat', 'lon'), may hold values from -30 to 30
- observed_state: bfloat16 [222, 320, 512], P(None, 'lat', 'lon'), may hold values from -30 to 30
- longterm_average_state: bfloat16 [222, 320, 512], P(None, 'lat', 'lon'), may hold values from -30 to 30
Outputs:
- blurred_mismatch_map: bfloat16 [222, 320, 512], P(None, 'lat', 'lon')
- quadratic_mean_mistake: float32 [222], replicated
- pattern_agreement: float32 [222], replicated
All inputs are finite; a program needn't handle non-finite values.
Results may differ from a plain program's by a relative error of at most 0.00155.
Values may be sent and summed in bfloat16 or wider, within the bound.
A program may use at most 128 MiB of HBM per device.

v0:
```python
import jax
import jax.numpy as jnp
from jax import lax
from jax.sharding import PartitionSpec as P

epsilon = 1e-06


def extended(cells, sides, width):
    for axis, dim in sides:
        count = lax.axis_size(axis)
        head = lax.slice_in_dim(cells, 0, width, axis=dim)
        tail = lax.slice_in_dim(cells, cells.shape[dim] - width, cells.shape[dim], axis=dim)
        cells = jnp.concatenate(
            [
                lax.ppermute(tail, axis, [(i, (i + 1) % count) for i in range(count)]),
                cells,
                lax.ppermute(head, axis, [((i + 1) % count, i) for i in range(count)]),
            ],
            axis=dim,
        )
    return cells


def deviation_from_normal(predicted_state, observed_state, longterm_average_state):
    normal_reference_state = longterm_average_state.astype(jnp.float32)
    return (
        predicted_state.astype(jnp.float32) - normal_reference_state,
        observed_state.astype(jnp.float32) - normal_reference_state,
    )


def vertical_sum(member):
    return member[:, :-2] + member[:, 1:-1] + member[:, 2:]


def horizontal_sum(member):
    return member[:, :, :-2] + member[:, :, 1:-1] + member[:, :, 2:]


def finish(running_accumulations, grid_cells):
    mean_fcst = running_accumulations[1] / grid_cells
    mean_true = running_accumulations[2] / grid_cells
    variance_fcst = running_accumulations[3] / grid_cells - mean_fcst * mean_fcst
    variance_true = running_accumulations[4] / grid_cells - mean_true * mean_true
    covariance = running_accumulations[5] / grid_cells - mean_fcst * mean_true
    quadratic_mean_mistake = jnp.sqrt(running_accumulations[0] / grid_cells)
    pattern_agreement = covariance / jnp.sqrt((variance_fcst + epsilon) * (variance_true + epsilon))
    return (quadratic_mean_mistake, pattern_agreement)


def local(predicted_state, observed_state, longterm_average_state):
    nearby_parallel_accumulated = predicted_state.shape[1]
    parallel_overall_accumulated = nearby_parallel_accumulated * lax.axis_size("lat")
    meridian_accumulated = predicted_state.shape[2] * lax.axis_size("lon")
    row_start = lax.axis_index("lat") * nearby_parallel_accumulated
    row_index = row_start + jnp.arange(nearby_parallel_accumulated, dtype=jnp.int32)
    stacked_inputs = jnp.stack([predicted_state, observed_state, longterm_average_state])
    rimmed = extended(stacked_inputs, (("lat", 2), ("lon", 3)), 1)
    widened = deviation_from_normal(rimmed[0], rimmed[1], rimmed[2])
    padded_index = row_start - 1 + jnp.arange(nearby_parallel_accumulated + 2, dtype=jnp.int32)
    inside = ((padded_index >= 0) & (padded_index < parallel_overall_accumulated)).astype(
        jnp.float32
    )[None, :, None]
    summed = tuple((horizontal_sum(vertical_sum(member * inside)) for member in widened))
    row_count = (
        3.0
        - (row_index == 0).astype(jnp.float32)
        - (row_index == parallel_overall_accumulated - 1).astype(jnp.float32)
    )
    divisor = (3.0 * row_count)[:, None]
    averaged_prediction = summed[0] / divisor
    averaged_observation = summed[1] / divisor
    prediction_mismatch = averaged_prediction - averaged_observation
    all_rows = jnp.arange(parallel_overall_accumulated, dtype=jnp.float32)
    cosine = jnp.cos(jnp.pi * (0.5 - all_rows / (parallel_overall_accumulated - 1)))
    weight_all = cosine / jnp.mean(cosine)
    cosine_factor_vector = lax.dynamic_slice_in_dim(
        weight_all, row_start, nearby_parallel_accumulated
    )[:, None]
    weighted_fcst = cosine_factor_vector * averaged_prediction
    weighted_true = cosine_factor_vector * averaged_observation
    running_accumulations = jnp.stack(
        [
            jnp.sum(cosine_factor_vector * prediction_mismatch * prediction_mismatch, axis=(1, 2)),
            jnp.sum(weighted_fcst, axis=(1, 2)),
            jnp.sum(weighted_true, axis=(1, 2)),
            jnp.sum(weighted_fcst * averaged_prediction, axis=(1, 2)),
            jnp.sum(weighted_true * averaged_observation, axis=(1, 2)),
            jnp.sum(weighted_fcst * averaged_observation, axis=(1, 2)),
        ]
    )
    totals = lax.psum(running_accumulations, ("lat", "lon"))
    quadratic_mean_mistake, pattern_agreement = finish(
        totals, float(parallel_overall_accumulated * meridian_accumulated)
    )
    return (prediction_mismatch.astype(jnp.bfloat16), quadratic_mean_mistake, pattern_agreement)


def solution(mesh):
    placed = (P(None, "lat", "lon"), P(None, "lat", "lon"), P(None, "lat", "lon"))
    return jax.shard_map(
        local,
        mesh=mesh,
        in_specs=placed,
        out_specs=(P(None, "lat", "lon"), P(), P()),
        check_vma=False,
    )
```

profile of v0, /device:TPU:0, one launch (start us, length us, event | category | flops | bytes accessed | tf_op | source)
XLA Modules:
  0.0 139.8 jit_solution(17298895487577244605)
XLA Ops:
  0.6 4.5 %copy.6 = bf16[222,40,128]{0,1,2:T(8,128)(2,1)S(1)} copy(bf16[222,40,128]{2,1,0:T(8,128)(2,1)} %param.3) | data formatting | bytes 4546560 | tf_op args[0]
  5.1 5.2 %copy.7 = bf16[222,40,128]{0,1,2:T(8,128)(2,1)} copy(bf16[222,40,128]{2,1,0:T(8,128)(2,1)} %param.4) | data formatting | bytes 4546560 | tf_op args[1]
  10.3 5.3 %copy.8 = bf16[222,40,128]{0,1,2:T(8,128)(2,1)} copy(bf16[222,40,128]{2,1,0:T(8,128)(2,1)} %param.5) | data formatting | bytes 4546560 | tf_op args[2]
  15.6 3.1 %pad_maximum_fusion.3 = (bf16[3,222,1,128]{1,2,3,0:T(2,128)(2,1)}, bf16[3,222,1,128]{1,2,3,0:T(2,128)(2,1)}) fusion(bf16[1,222,40,128]{1,2,3,0:T(8,128)(2,1)} %bitcast.25, bf16[1,222,40,128]{1,2,3,0:T(8,128)(2,1)} %bitcast.22, bf16[1,222,40,128]{1,2,3,0:T(8,128)(2,1)S(1)} %bitcast.19), kind=kLoop, calls=%fused_computation.30 | loop fusion | flops 1022976 | bytes 7160832 | tf_op jit(solution)/shard_map/slice | solution.py:13
  18.7 3.0 %collective-permute-start = (bf16[3,222,1,128]{1,2,3,0:T(2,128)(2,1)}, bf16[3,222,1,128]{1,2,3,0:T(2,128)(2,1)S(1)}, u32[]{:S(2)}, u32[]{:S(2)}) collective-permute-start(bf16[3,222,1,128]{1,2,3,0:T(2,128)(2,1)} %get-tuple-element.18), channel_id=1, source_target_pairs={{0,4},{4,8},{8,12},{12,16},{16,20},{20,24},{24,28},{28,0},{1,5},{5... | collective-permute-start | bytes 511496 | tf_op jit(solution)/shard_map/ppermute | solution.py:16
  21.7 3.0 %collective-permute-start.1 = (bf16[3,222,1,128]{1,2,3,0:T(2,128)(2,1)}, bf16[3,222,1,128]{1,2,3,0:T(2,128)(2,1)S(1)}, u32[]{:S(2)}, u32[]{:S(2)}) collective-permute-start(bf16[3,222,1,128]{1,2,3,0:T(2,128)(2,1)} %get-tuple-element.19), channel_id=1, source_target_pairs={{4,0},{8,4},{12,8},{16,12},{20,16},{24,20},{28,24},{0,28},{5,1},{9... | collective-permute-start | bytes 511496 | tf_op jit(solution)/shard_map/ppermute | solution.py:18
  24.8 0.7 fusion.11
  26.1 0.5 fusion.19
  26.6 0.6 fusion.10
  27.2 11.6 %collective-permute-done = bf16[3,222,1,128]{1,2,3,0:T(2,128)(2,1)S(1)} collective-permute-done((bf16[3,222,1,128]{1,2,3,0:T(2,128)(2,1)}, bf16[3,222,1,128]{1,2,3,0:T(2,128)(2,1)S(1)}, u32[]{:S(2)}, u32[]{:S(2)}) %collective-permute-start) | collective-permute-done | bytes 170528 | tf_op jit(solution)/shard_map/ppermute | solution.py:16
  38.8 2.1 %collective-permute-done.1 = bf16[3,222,1,128]{1,2,3,0:T(2,128)(2,1)S(1)} collective-permute-done((bf16[3,222,1,128]{1,2,3,0:T(2,128)(2,1)}, bf16[3,222,1,128]{1,2,3,0:T(2,128)(2,1)S(1)}, u32[]{:S(2)}, u32[]{:S(2)}) %collective-permute-start.1) | collective-permute-done | bytes 170528 | tf_op jit(solution)/shard_map/ppermute | solution.py:18
  40.9 1.5 %pad_maximum_fusion.8 = (bf16[3,222,42,1]{1,2,3,0:T(8,128)(2,1)}, bf16[3,222,42,1]{1,2,3,0:T(8,128)(2,1)}) fusion(bf16[3,222,1,128]{1,2,3,0:T(2,128)(2,1)S(1)} %collective-permute-done.1, bf16[3,222,1,128]{1,2,3,0:T(2,128)(2,1)S(1)} %collective-permute-done, bf16[1,222,40,128]{1,2,3,0:T(8,128)(2,1)} %bitcast.26, bf16[1,222,40,128]{1,2,3,0:T(8,128)(2,1)} %bitcast.23, ...), kind=kLoop, calls=%fused_computation.35 | loop fusion | flops 559440 | bytes 7272720 | tf_op jit(solution)/shard_map/slice | solution.py:13
  42.4 0.0 collective-permute-start.2
  42.4 1.7 %collective-permute-start.3 = (bf16[3,222,42,1]{1,2,3,0:T(8,128)(2,1)}, bf16[3,222,42,1]{1,2,3,0:T(8,128)(2,1)S(1)}, u32[]{:S(2)}, u32[]{:S(2)}) collective-permute-start(bf16[3,222,42,1]{1,2,3,0:T(8,128)(2,1)} %get-tuple-element.17), channel_id=1, source_target_pairs={{1,0},{2,1},{3,2},{0,3},{5,4},{6,5},{7,6},{4,7},{9,8},{10,9},{11,1... | collective-permute-start | bytes 167840 | tf_op jit(solution)/shard_map/ppermute | solution.py:18
  44.2 0.5 and_convert_fusion
  44.7 0.7 dynamic_slice.3
  45.4 0.0 copy-start.1
  45.4 1.0 collective-permute-done.2
  46.4 0.1 collective-permute-done.3
  46.5 10.1 %pad_maximum_fusion = bf16[3,222,42,130]{1,2,3,0:T(8,128)(2,1)S(1)} fusion(bf16[3,222,42,1]{1,2,3,0:T(8,128)(2,1)S(1)} %collective-permute-done.3, bf16[3,222,1,128]{1,2,3,0:T(2,128)(2,1)S(1)} %collective-permute-done.1, bf16[1,222,40,128]{1,2,3,0:T(8,128)(2,1)} %bitcast.27, bf16[1,222,40,128]{1,2,3,0:T(8,128)(2,1)} %bitcast.24, ...), kind=kLoop, calls=%fused_computation | loop fusion | flops 50909040 | bytes 14545440 | tf_op jit(solution)/shard_map/concatenate | solution.py:14
  56.6 0.0 copy-done.1
  56.6 5.5 %fusion.1 = (f32[222,42,130]{0,1,2:T(8,128)}, f32[222,42,130]{0,1,2:T(8,128)}) fusion(bf16[3,222,42,130]{1,2,3,0:T(8,128)(2,1)S(1)} %pad_maximum_fusion, f32[42]{0:T(128)S(1)} %copy-done.1), kind=kLoop, calls=%fused_computation.10 | loop fusion | flops 8484840 | bytes 16969848 | tf_op jit(solution)/shard_map/mul | solution.py:65
  62.1 0.0 copy-start
  62.1 16.3 %slice_add_fusion = (f32[222,40,130]{0,1,2:T(8,128)S(1)}, f32[222,40,130]{0,1,2:T(8,128)}) fusion(f32[222,42,130]{0,1,2:T(8,128)} %get-tuple-element.15, f32[222,42,130]{0,1,2:T(8,128)} %get-tuple-element.14), kind=kLoop, calls=%fused_computation.13 | loop fusion | flops 4617600 | bytes 36940800 | tf_op jit(solution)/shard_map/add | solution.py:34
  78.4 0.0 copy-done
  78.4 12.7 %fusion.5 = (f32[222]{0:T(256)S(1)}, f32[222]{0:T(256)S(1)}, f32[222]{0:T(256)S(1)}, f32[222]{0:T(256)S(1)}, f32[222]{0:T(256)S(1)}, /*index=5*/f32[222]{0:T(256...) fusion(f32[40]{0:T(128)S(1)} %dynamic_slice.3, f32[40]{0:T(128)S(1)} %copy-done, f32[222,40,130]{0,1,2:T(8,128)S(1)} %get-tuple-element.22, ...), kind=kLoop, calls=%fused_computation.18 | loop fusion | flops 22731468 | bytes 36378128 | tf_op jit(solution)/shard_map/reduce_sum | solution.py:90
  91.1 39.4 %psum.7 = f32[6,222]{1,0:T(8,128)S(1)} all-reduce(f32[6,222]{1,0:T(8,128)S(1)} %stack.43), channel_id=1, replica_groups=mesh['lat'=8,'lon'=4] {'lat','lon'}, use_global_device_ids=true, to_apply=%region_7.0 | all-reduce | flops 1332 | bytes 10656 | tf_op jit(solution)/shard_map/psum | solution.py:93
  130.5 0.6 fusion.15
  131.1 4.9 %subtract_convert_fusion = bf16[222,40,128]{0,1,2:T(8,128)(2,1)S(1)} fusion(f32[222,40,128]{0,1,2:T(8,128)} %get-tuple-element.13, f32[222,40,128]{0,1,2:T(8,128)} %get-tuple-element.12), kind=kLoop, calls=%fused_computation.27 | loop fusion | flops 2273280 | bytes 11366400 | tf_op jit(solution)/shard_map/convert_element_type | solution.py:97
  136.0 3.8 %copy.9 = bf16[222,40,128]{2,1,0:T(8,128)(2,1)} copy(bf16[222,40,128]{0,1,2:T(8,128)(2,1)S(1)} %subtract_convert_fusion) | data formatting | bytes 4546560
  (1 shorter events, 0.0 us)
Async XLA Ops:
  18.7 20.1 %collective-permute-start = (bf16[3,222,1,128]{1,2,3,0:T(2,128)(2,1)}, bf16[3,222,1,128]{1,2,3,0:T(2,128)(2,1)S(1)}, u32[]{:S(2)}, u32[]{:S(2)}) collective-permute-start(bf16[3,222,1,128]{1,2,3,0:T(2,128)(2,1)} %get-tuple-element.18), channel_id=1, source_target_pairs={{0,4},{4,8},{8,12},{12,16},{16,20},{20,24},{24,28},{28,0},{1,5},{5... | collective-permute-start | bytes 511496 | tf_op jit(solution)/shard_map/ppermute | solution.py:16
  21.7 19.2 %collective-permute-start.1 = (bf16[3,222,1,128]{1,2,3,0:T(2,128)(2,1)}, bf16[3,222,1,128]{1,2,3,0:T(2,128)(2,1)S(1)}, u32[]{:S(2)}, u32[]{:S(2)}) collective-permute-start(bf16[3,222,1,128]{1,2,3,0:T(2,128)(2,1)} %get-tuple-element.19), channel_id=1, source_target_pairs={{4,0},{8,4},{12,8},{16,12},{20,16},{24,20},{28,24},{0,28},{5,1},{9... | collective-permute-start | bytes 511496 | tf_op jit(solution)/shard_map/ppermute | solution.py:18
  42.4 4.0 %collective-permute-start.2 = (bf16[3,222,42,1]{1,2,3,0:T(8,128)(2,1)}, bf16[3,222,42,1]{1,2,3,0:T(8,128)(2,1)S(1)}, u32[]{:S(2)}, u32[]{:S(2)}) collective-permute-start(bf16[3,222,42,1]{1,2,3,0:T(8,128)(2,1)} %get-tuple-element.16), channel_id=1, source_target_pairs={{0,1},{1,2},{2,3},{3,0},{4,5},{5,6},{6,7},{7,4},{8,9},{9,10},{10,1... | collective-permute-start | bytes 167840 | tf_op jit(solution)/shard_map/ppermute | solution.py:16
  42.4 4.0 %collective-permute-start.3 = (bf16[3,222,42,1]{1,2,3,0:T(8,128)(2,1)}, bf16[3,222,42,1]{1,2,3,0:T(8,128)(2,1)S(1)}, u32[]{:S(2)}, u32[]{:S(2)}) collective-permute-start(bf16[3,222,42,1]{1,2,3,0:T(8,128)(2,1)} %get-tuple-element.17), channel_id=1, source_target_pairs={{1,0},{2,1},{3,2},{0,3},{5,4},{6,5},{7,6},{4,7},{9,8},{10,9},{11,1... | collective-permute-start | bytes 167840 | tf_op jit(solution)/shard_map/ppermute | solution.py:18
  45.4 11.1 %copy-start.1 = (f32[42]{0:T(128)S(1)}, f32[42]{0:T(128)}, u32[]{:S(2)}) copy-start(f32[42]{0:T(128)} %and_convert_fusion) | copy-start | bytes 508
  62.1 16.3 %copy-start = (f32[40]{0:T(128)S(1)}, f32[40]{0:T(128)}, u32[]{:S(2)}) copy-start(f32[40]{0:T(128)} %fusion.19) | copy-start | bytes 484
where the time goes:
time: 140 us
  other arithmetic  57 us (41%)
  blocking collectives  39.4 us (28%)
  local copies, waits for them, and re-layouts  19.5 us (14%)
  waiting for transfers between devices  14.7 us (10%)
  starting transfers between devices  7.78 us (6%)
    psum x1, blocking collectives, local(): totals = lax.psum(running_accumulations, ('lat', 'lon'))  39.4 us
    unnamed x8, local copies, waits for them, and re-layouts  18.7 us
    add x1, other arithmetic, vertical_sum(): return member[:, :-2] + member[:, 1:-1] + member[:, 2:]  16.3 us
    reduce_sum x1, other arithmetic, local(): jnp.sum(weighted_fcst * averaged_observation, axis=(1, 2))  12.7 us
    ppermute x2, waiting for transfers between devices, extended(): lax.ppermute(tail, axis, [(i, (i + 1) % count) for i in range(count)])  12.6 us
    concatenate x1, other arithmetic, extended(): jnp.concatenate([lax.ppermute(tail, axis, [(i, (i + 1) % count) for i in...  10.1 us
    mul x1, other arithmetic, local(): member * inside  5.51 us
    convert_element_type x1, other arithmetic, local(): prediction_mismatch.astype(jnp.bfloat16)  4.93 us
  transfers between devices with their start and end apart: 4, of which 4 were waited for; matrix products, arithmetic and copies ran while one was open for 2% of the time, Pallas kernels for 0%

commit v1 on v0

--- a/solution.py
+++ b/solution.py
@@ -90,7 +90,8 @@
             jnp.sum(weighted_fcst * averaged_observation, axis=(1, 2)),
         ]
     )
-    totals = lax.psum(running_accumulations, ("lat", "lon"))
+    signs_end = lambda vector: jax.lax.psum(jax.lax.psum(vector, "lat"), "lon")
+    totals = signs_end(running_accumulations)
     quadratic_mean_mistake, pattern_agreement = finish(
         totals, float(parallel_overall_accumulated * meridian_accumulated)
     )

time: 140 us -> 127 us (0.907)
  blocking collectives: 39.4 us -> 26.5 us
    psum x1 -> x2, blocking collectives: 39.4 us -> 26.5 us  [local(): signs_end = lambda vector: jax.lax.psum(jax.lax.psum(vector, 'lat'), 'lon')]
where the time goes in v1:
time: 127 us
  other arithmetic  57 us (45%)
  blocking collectives  26.5 us (21%)
  local copies, waits for them, and re-layouts  19.5 us (15%)
  waiting for transfers between devices  14.7 us (12%)
  starting transfers between devices  7.78 us (6%)
  between operations  1.34 us (1%)
    psum x2, blocking collectives, local(): signs_end = lambda vector: jax.lax.psum(jax.lax.psum(vector, 'lat'), 'lon')  26.5 us
    unnamed x8, local copies, waits for them, and re-layouts  18.7 us
    add x1, other arithmetic, vertical_sum(): return member[:, :-2] + member[:, 1:-1] + member[:, 2:]  16.3 us
    reduce_sum x1, other arithmetic, local(): jnp.sum(weighted_fcst * averaged_observation, axis=(1, 2))  12.7 us
    ppermute x2, waiting for transfers between devices, extended(): lax.ppermute(tail, axis, [(i, (i + 1) % count) for i in range(count)])  12.6 us
    concatenate x1, other arithmetic, extended(): jnp.concatenate([lax.ppermute(tail, axis, [(i, (i + 1) % count) for i in...  10.1 us
    mul x1, other arithmetic, local(): member * inside  5.51 us
    convert_element_type x1, other arithmetic, local(): prediction_mismatch.astype(jnp.bfloat16)  4.93 us
  transfers between devices with their start and end apart: 4, of which 4 were waited for; matrix products, arithmetic and copies ran while one was open for 2% of the time, Pallas kernels for 0%

profile of v1, /device:TPU:0, one launch (start us, length us, event | category | flops | bytes accessed | tf_op | source)
XLA Modules:
  0.0 126.9 jit_solution(17834801807765138627)
XLA Ops:
  0.6 4.5 %copy.6 = bf16[222,40,128]{0,1,2:T(8,128)(2,1)S(1)} copy(bf16[222,40,128]{2,1,0:T(8,128)(2,1)} %param.3) | data formatting | bytes 4546560 | tf_op args[0]
  5.1 5.2 %copy.7 = bf16[222,40,128]{0,1,2:T(8,128)(2,1)} copy(bf16[222,40,128]{2,1,0:T(8,128)(2,1)} %param.4) | data formatting | bytes 4546560 | tf_op args[1]
  10.3 5.3 %copy.8 = bf16[222,40,128]{0,1,2:T(8,128)(2,1)} copy(bf16[222,40,128]{2,1,0:T(8,128)(2,1)} %param.5) | data formatting | bytes 4546560 | tf_op args[2]
  15.6 3.1 %pad_maximum_fusion.3 = (bf16[3,222,1,128]{1,2,3,0:T(2,128)(2,1)}, bf16[3,222,1,128]{1,2,3,0:T(2,128)(2,1)}) fusion(bf16[1,222,40,128]{1,2,3,0:T(8,128)(2,1)} %bitcast.25, bf16[1,222,40,128]{1,2,3,0:T(8,128)(2,1)} %bitcast.22, bf16[1,222,40,128]{1,2,3,0:T(8,128)(2,1)S(1)} %bitcast.19), kind=kLoop, calls=%fused_computation.30 | loop fusion | flops 1022976 | bytes 7160832 | tf_op jit(solution)/shard_map/slice | solution.py:13
  18.7 3.0 %collective-permute-start = (bf16[3,222,1,128]{1,2,3,0:T(2,128)(2,1)}, bf16[3,222,1,128]{1,2,3,0:T(2,128)(2,1)S(1)}, u32[]{:S(2)}, u32[]{:S(2)}) collective-permute-start(bf16[3,222,1,128]{1,2,3,0:T(2,128)(2,1)} %get-tuple-element.18), channel_id=1, source_target_pairs={{0,4},{4,8},{8,12},{12,16},{16,20},{20,24},{24,28},{28,0},{1,5},{5... | collective-permute-start | bytes 511496 | tf_op jit(solution)/shard_map/ppermute | solution.py:16
  21.7 3.0 %collective-permute-start.1 = (bf16[3,222,1,128]{1,2,3,0:T(2,128)(2,1)}, bf16[3,222,1,128]{1,2,3,0:T(2,128)(2,1)S(1)}, u32[]{:S(2)}, u32[]{:S(2)}) collective-permute-start(bf16[3,222,1,128]{1,2,3,0:T(2,128)(2,1)} %get-tuple-element.19), channel_id=1, source_target_pairs={{4,0},{8,4},{12,8},{16,12},{20,16},{24,20},{28,24},{0,28},{5,1},{9... | collective-permute-start | bytes 511496 | tf_op jit(solution)/shard_map/ppermute | solution.py:18
  24.8 0.7 fusion.11
  26.1 0.5 fusion.19
  26.6 0.6 fusion.10
  27.2 11.6 %collective-permute-done = bf16[3,222,1,128]{1,2,3,0:T(2,128)(2,1)S(1)} collective-permute-done((bf16[3,222,1,128]{1,2,3,0:T(2,128)(2,1)}, bf16[3,222,1,128]{1,2,3,0:T(2,128)(2,1)S(1)}, u32[]{:S(2)}, u32[]{:S(2)}) %collective-permute-start) | collective-permute-done | bytes 170528 | tf_op jit(solution)/shard_map/ppermute | solution.py:16
  38.8 2.1 %collective-permute-done.1 = bf16[3,222,1,128]{1,2,3,0:T(2,128)(2,1)S(1)} collective-permute-done((bf16[3,222,1,128]{1,2,3,0:T(2,128)(2,1)}, bf16[3,222,1,128]{1,2,3,0:T(2,128)(2,1)S(1)}, u32[]{:S(2)}, u32[]{:S(2)}) %collective-permute-start.1) | collective-permute-done | bytes 170528 | tf_op jit(solution)/shard_map/ppermute | solution.py:18
  40.9 1.5 %pad_maximum_fusion.8 = (bf16[3,222,42,1]{1,2,3,0:T(8,128)(2,1)}, bf16[3,222,42,1]{1,2,3,0:T(8,128)(2,1)}) fusion(bf16[3,222,1,128]{1,2,3,0:T(2,128)(2,1)S(1)} %collective-permute-done.1, bf16[3,222,1,128]{1,2,3,0:T(2,128)(2,1)S(1)} %collective-permute-done, bf16[1,222,40,128]{1,2,3,0:T(8,128)(2,1)} %bitcast.26, bf16[1,222,40,128]{1,2,3,0:T(8,128)(2,1)} %bitcast.23, ...), kind=kLoop, calls=%fused_computation.35 | loop fusion | flops 559440 | bytes 7272720 | tf_op jit(solution)/shard_map/slice | solution.py:13
  42.4 0.0 collective-permute-start.2
  42.4 1.7 %collective-permute-start.3 = (bf16[3,222,42,1]{1,2,3,0:T(8,128)(2,1)}, bf16[3,222,42,1]{1,2,3,0:T(8,128)(2,1)S(1)}, u32[]{:S(2)}, u32[]{:S(2)}) collective-permute-start(bf16[3,222,42,1]{1,2,3,0:T(8,128)(2,1)} %get-tuple-element.17), channel_id=1, source_target_pairs={{1,0},{2,1},{3,2},{0,3},{5,4},{6,5},{7,6},{4,7},{9,8},{10,9},{11,1... | collective-permute-start | bytes 167840 | tf_op jit(solution)/shard_map/ppermute | solution.py:18
  44.2 0.5 and_convert_fusion
  44.7 0.7 dynamic_slice.3
  45.4 0.0 copy-start.1
  45.4 1.0 collective-permute-done.2
  46.4 0.1 collective-permute-done.3
  46.5 10.1 %pad_maximum_fusion = bf16[3,222,42,130]{1,2,3,0:T(8,128)(2,1)S(1)} fusion(bf16[3,222,42,1]{1,2,3,0:T(8,128)(2,1)S(1)} %collective-permute-done.3, bf16[3,222,1,128]{1,2,3,0:T(2,128)(2,1)S(1)} %collective-permute-done.1, bf16[1,222,40,128]{1,2,3,0:T(8,128)(2,1)} %bitcast.27, bf16[1,222,40,128]{1,2,3,0:T(8,128)(2,1)} %bitcast.24, ...), kind=kLoop, calls=%fused_computation | loop fusion | flops 50909040 | bytes 14545440 | tf_op jit(solution)/shard_map/concatenate | solution.py:14
  56.6 0.0 copy-done.1
  56.6 5.5 %fusion.1 = (f32[222,42,130]{0,1,2:T(8,128)}, f32[222,42,130]{0,1,2:T(8,128)}) fusion(bf16[3,222,42,130]{1,2,3,0:T(8,128)(2,1)S(1)} %pad_maximum_fusion, f32[42]{0:T(128)S(1)} %copy-done.1), kind=kLoop, calls=%fused_computation.10 | loop fusion | flops 8484840 | bytes 16969848 | tf_op jit(solution)/shard_map/mul | solution.py:65
  62.1 0.0 copy-start
  62.1 16.3 %slice_add_fusion = (f32[222,40,130]{0,1,2:T(8,128)S(1)}, f32[222,40,130]{0,1,2:T(8,128)}) fusion(f32[222,42,130]{0,1,2:T(8,128)} %get-tuple-element.15, f32[222,42,130]{0,1,2:T(8,128)} %get-tuple-element.14), kind=kLoop, calls=%fused_computation.13 | loop fusion | flops 4617600 | bytes 36940800 | tf_op jit(solution)/shard_map/add | solution.py:34
  78.4 0.0 copy-done
  78.4 12.7 %fusion.5 = (f32[222]{0:T(256)S(1)}, f32[222]{0:T(256)S(1)}, f32[222]{0:T(256)S(1)}, f32[222]{0:T(256)S(1)}, f32[222]{0:T(256)S(1)}, /*index=5*/f32[222]{0:T(256...) fusion(f32[40]{0:T(128)S(1)} %dynamic_slice.3, f32[40]{0:T(128)S(1)} %copy-done, f32[222,40,130]{0,1,2:T(8,128)S(1)} %get-tuple-element.22, ...), kind=kLoop, calls=%fused_computation.18 | loop fusion | flops 22731468 | bytes 36378128 | tf_op jit(solution)/shard_map/reduce_sum | solution.py:90
  91.1 20.7 %psum.14 = f32[6,222]{1,0:T(8,128)S(1)} all-reduce(f32[6,222]{1,0:T(8,128)S(1)} %stack.43), channel_id=1, replica_groups=mesh['lat'=8,'lon'=4] {'lat'}, use_global_device_ids=true, to_apply=%region_7.0 | all-reduce | flops 1332 | bytes 10656 | tf_op jit(solution)/shard_map/psum | solution.py:93
  111.8 5.8 %psum.15 = f32[6,222]{1,0:T(8,128)S(1)} all-reduce(f32[6,222]{1,0:T(8,128)S(1)} %psum.14), channel_id=1, replica_groups=mesh['lat'=8,'lon'=4] {'lon'}, use_global_device_ids=true, to_apply=%region_8.0 | all-reduce | flops 1332 | bytes 10656 | tf_op jit(solution)/shard_map/psum | solution.py:93
  117.6 0.6 fusion.15
  118.1 4.9 %subtract_convert_fusion = bf16[222,40,128]{0,1,2:T(8,128)(2,1)S(1)} fusion(f32[222,40,128]{0,1,2:T(8,128)} %get-tuple-element.13, f32[222,40,128]{0,1,2:T(8,128)} %get-tuple-element.12), kind=kLoop, calls=%fused_computation.27 | loop fusion | flops 2273280 | bytes 11366400 | tf_op jit(solution)/shard_map/convert_element_type | solution.py:98
  123.1 3.8 %copy.9 = bf16[222,40,128]{2,1,0:T(8,128)(2,1)} copy(bf16[222,40,128]{0,1,2:T(8,128)(2,1)S(1)} %subtract_convert_fusion) | data formatting | bytes 4546560
  (1 shorter events, 0.0 us)
Async XLA Ops:
  18.7 20.1 %collective-permute-start = (bf16[3,222,1,128]{1,2,3,0:T(2,128)(2,1)}, bf16[3,222,1,128]{1,2,3,0:T(2,128)(2,1)S(1)}, u32[]{:S(2)}, u32[]{:S(2)}) collective-permute-start(bf16[3,222,1,128]{1,2,3,0:T(2,128)(2,1)} %get-tuple-element.18), channel_id=1, source_target_pairs={{0,4},{4,8},{8,12},{12,16},{16,20},{20,24},{24,28},{28,0},{1,5},{5... | collective-permute-start | bytes 511496 | tf_op jit(solution)/shard_map/ppermute | solution.py:16
  21.7 19.2 %collective-permute-start.1 = (bf16[3,222,1,128]{1,2,3,0:T(2,128)(2,1)}, bf16[3,222,1,128]{1,2,3,0:T(2,128)(2,1)S(1)}, u32[]{:S(2)}, u32[]{:S(2)}) collective-permute-start(bf16[3,222,1,128]{1,2,3,0:T(2,128)(2,1)} %get-tuple-element.19), channel_id=1, source_target_pairs={{4,0},{8,4},{12,8},{16,12},{20,16},{24,20},{28,24},{0,28},{5,1},{9... | collective-permute-start | bytes 511496 | tf_op jit(solution)/shard_map/ppermute | solution.py:18
  42.4 4.0 %collective-permute-start.2 = (bf16[3,222,42,1]{1,2,3,0:T(8,128)(2,1)}, bf16[3,222,42,1]{1,2,3,0:T(8,128)(2,1)S(1)}, u32[]{:S(2)}, u32[]{:S(2)}) collective-permute-start(bf16[3,222,42,1]{1,2,3,0:T(8,128)(2,1)} %get-tuple-element.16), channel_id=1, source_target_pairs={{0,1},{1,2},{2,3},{3,0},{4,5},{5,6},{6,7},{7,4},{8,9},{9,10},{10,1... | collective-permute-start | bytes 167840 | tf_op jit(solution)/shard_map/ppermute | solution.py:16
  42.4 4.0 %collective-permute-start.3 = (bf16[3,222,42,1]{1,2,3,0:T(8,128)(2,1)}, bf16[3,222,42,1]{1,2,3,0:T(8,128)(2,1)S(1)}, u32[]{:S(2)}, u32[]{:S(2)}) collective-permute-start(bf16[3,222,42,1]{1,2,3,0:T(8,128)(2,1)} %get-tuple-element.17), channel_id=1, source_target_pairs={{1,0},{2,1},{3,2},{0,3},{5,4},{6,5},{7,6},{4,7},{9,8},{10,9},{11,1... | collective-permute-start | bytes 167840 | tf_op jit(solution)/shard_map/ppermute | solution.py:18
  45.4 11.1 %copy-start.1 = (f32[42]{0:T(128)S(1)}, f32[42]{0:T(128)}, u32[]{:S(2)}) copy-start(f32[42]{0:T(128)} %and_convert_fusion) | copy-start | bytes 508
  62.1 16.3 %copy-start = (f32[40]{0:T(128)S(1)}, f32[40]{0:T(128)}, u32[]{:S(2)}) copy-start(f32[40]{0:T(128)} %fusion.19) | copy-start | bytes 484
